TPU v7x, 32 devices: a whole 2x2x4 slice. The times are simulated.
32 devices in a mesh: gx: 4 (over y, core), gy: 2 (over x), gz: 4 (over z).
Axes of the slice: x: 2, y: 2, z: 4, core: 2. Of those that a mesh axis runs over, the one named last changes fastest.
Arguments:
- tokens: bfloat16 [32, 6144], P('gy'), may hold values from -6 to 6
- route: int32 [32, 2], P('gy'), may hold values from 0 to 3, all different within a row; in each aligned block of 16 rows (0 to 15, 16 to 31, ...) at most 12 rows name the same one
- weight_q: int32 [32, 2], P('gy'), may hold values from 1 to 65535
- w_gate: bfloat16 [4, 6144, 16384], P('gx', 'gy', 'gz'), may hold values from -0.078125 to 0.078125
- w_up: bfloat16 [4, 6144, 16384], P('gx', 'gy', 'gz'), may hold values from -0.078125 to 0.078125
- w_down: bfloat16 [4, 16384, 6144], P('gx', 'gz', 'gy'), may hold values from -0.046875 to 0.046875
Outputs:
- mixed: bfloat16 [32, 6144], P('gy', ('gx', 'gz'))
Inputs may be any that keep to these rules, and one draw needn't show every extreme that they name: `route`: the 2 entries of a row are different; in each block of 16 rows owned by one index of gy no expert is named by more than 12 rows, a bound that some block reaches.
All inputs are finite; a program needn't handle non-finite values.
Results may differ from a plain program's by a relative error of at most 0.0049.
Values may be sent and summed in bfloat16 or wider, within the bound.
A program may use at most 256 MiB of HBM per device.

v0:
```python
import jax
import jax.numpy as jnp
from jax import lax
from jax.sharding import PartitionSpec as P

CAP = 12


def per_device(tokens, route, weight_q, w_gate, w_up, w_down):
    expert = lax.axis_index("gx")
    width_z = lax.axis_size("gz")
    owners = lax.axis_size("gy")
    hits = (route == expert).astype(jnp.int32)
    routed = jnp.sum(hits, axis=1)
    slot_index = jnp.cumsum(routed) - 1
    columns = jnp.arange(CAP, dtype=jnp.int32)
    placing = (slot_index[None, :] == columns[:, None]) & (routed[None, :] > 0)
    place_half = placing.astype(jnp.bfloat16)
    place_full = placing.astype(jnp.float32)
    outgoing = jnp.dot(place_half, tokens, preferred_element_type=jnp.float32).astype(jnp.bfloat16)
    weights_f = weight_q.astype(jnp.float32)
    shares = weights_f / jnp.sum(weights_f, axis=1, keepdims=True)
    token_gate = jnp.sum(hits.astype(jnp.float32) * shares, axis=1)
    slot_gate = jnp.dot(place_full, token_gate, precision=lax.Precision.HIGHEST)
    gate_slab, up_slab = (
        lax.all_to_all(w_gate[0], "gy", split_axis=1, concat_axis=0, tiled=True),
        lax.all_to_all(w_up[0], "gy", split_axis=1, concat_axis=0, tiled=True),
    )
    piece = lax.all_gather(outgoing, "gy", axis=0, tiled=True)
    gate = jnp.dot(piece, gate_slab, preferred_element_type=jnp.float32)
    upper = jnp.dot(piece, up_slab, preferred_element_type=jnp.float32)
    hidden = (jax.nn.silu(gate) * upper).astype(jnp.bfloat16)
    down_local = w_down[0]
    partial_value = jnp.dot(
        lax.all_gather(hidden, "gy", axis=1, tiled=True),
        down_local,
        preferred_element_type=jnp.float32,
    )
    portion = CAP // width_z
    column_width = partial_value.shape[1]
    blocks = partial_value.reshape(owners, width_z, portion, column_width)
    narrowed = lax.psum_scatter(blocks, "gz", scatter_dimension=1, tiled=True)
    arrived = lax.all_to_all(narrowed, "gy", split_axis=0, concat_axis=1, tiled=True)
    full = jnp.transpose(arrived[0], (1, 0, 2)).reshape(portion, owners * column_width)
    first = lax.axis_index("gz") * portion
    gate_part = lax.dynamic_slice_in_dim(slot_gate, first, portion, 0)
    place_part = lax.dynamic_slice_in_dim(place_full, first, portion, 0)
    weighted = gate_part[:, None] * full
    contribution = jnp.dot(place_part.T, weighted, precision=lax.Precision.HIGHEST)
    result = lax.psum_scatter(contribution, ("gx", "gz"), scatter_dimension=1, tiled=True)
    return result.astype(jnp.bfloat16)


def solution(mesh):
    in_specs = (
        P("gy", None),
        P("gy", None),
        P("gy", None),
        P("gx", "gy", "gz"),
        P("gx", "gy", "gz"),
        P("gx", "gz", "gy"),
    )
    out_specs = P("gy", ("gx", "gz"))
    return jax.shard_map(
        per_device, mesh=mesh, in_specs=in_specs, out_specs=out_specs, check_vma=False
    )
```

profile of v0, /device:TPU:0, one launch (start us, length us, event | category | flops | bytes accessed | tf_op | source)
XLA Modules:
  0.0 822.6 jit_solution(7426309213816833088)
XLA Ops:
  6.5 0.0 copy-start
  6.5 32.7 %copy.36 = bf16[1,3072,4096]{1,2,0:T(8,128)(2,1)} copy(bf16[1,3072,4096]{2,1,0:T(8,128)(2,1)} %param.9) | data formatting | bytes 50331648 | tf_op args[3]
  39.2 11.8 %all-to-all-start = ((bf16[3072,2,2048]{0,2,1:T(8,128)(2,1)}), bf16[3072,2,2048]{0,2,1:T(8,128)(2,1)}, u32[]{:S(2)}, u32[]{:S(2)}) async-start(bf16[3072,2,2048]{0,2,1:T(8,128)(2,1)} %bitcast.37), calls=%async_computation | async-start | bytes 50331648 | tf_op jit(solution)/shard_map/all_to_all | solution.py:26
  51.0 32.7 %copy.38 = bf16[1,3072,4096]{1,2,0:T(8,128)(2,1)} copy(bf16[1,3072,4096]{2,1,0:T(8,128)(2,1)} %param.10) | data formatting | bytes 50331648 | tf_op args[4]
  83.7 240.8 %all-to-all-done = bf16[3072,2,2048]{0,2,1:T(8,128)(2,1)} async-done(((bf16[3072,2,2048]{0,2,1:T(8,128)(2,1)}), bf16[3072,2,2048]{0,2,1:T(8,128)(2,1)}, u32[]{:S(2)}, u32[]{:S(2)}) %all-to-all-start) | async-done | bytes 25165856 | tf_op jit(solution)/shard_map/all_to_all | solution.py:26
  324.5 0.0 copy-start.2
  324.5 0.0 copy-start.4
  324.5 0.0 copy-start.3
  324.5 11.9 %all-to-all-start.1 = ((bf16[3072,2,2048]{0,2,1:T(8,128)(2,1)}), bf16[3072,2,2048]{0,2,1:T(8,128)(2,1)}, u32[]{:S(2)}, u32[]{:S(2)}) async-start(bf16[3072,2,2048]{0,2,1:T(8,128)(2,1)} %bitcast.36), calls=%async_computation.1 | async-start | bytes 50331648 | tf_op jit(solution)/shard_map/all_to_all | solution.py:27
  336.5 0.0 all-reduce.3.cloned.1.call-start
  336.5 0.0 copy-done.2
  336.6 0.1 copy.35
  336.7 0.1 add_reduce_fusion
  336.8 0.0 copy-done
  336.8 0.2 fusion.2
  337.0 275.4 %all-gather = bf16[2,12,6144]{2,1,0:T(8,128)(2,1)S(1)} all-gather(bf16[1,12,6144]{2,1,0:T(8,128)(2,1)S(1)} %fusion.2), channel_id=1, replica_groups=mesh['gx'=4,'gy'=2,'gz'=4] {'gy'}, dimensions={0}, use_global_device_ids=true | all-gather | bytes 442368 | tf_op jit(solution)/shard_map/all_gather | solution.py:29
  612.4 0.1 reshape.53
  612.5 0.0 copy-done.4
  612.5 0.6 dynamic-slice
  613.1 0.0 copy-done.3
  613.1 31.6 %copy.37 = bf16[2,3072,2048]{2,1,0:T(8,128)(2,1)} copy(bf16[2,3072,2048]{1,2,0:T(8,128)(2,1)} %bitcast.5) | data formatting | bytes 50331648 | tf_op jit(solution)/shard_map/all_to_all | solution.py:26
  644.7 0.0 all-to-all-done.1
  644.7 32.7 %copy.39 = bf16[2,3072,2048]{2,1,0:T(8,128)(2,1)} copy(bf16[2,3072,2048]{1,2,0:T(8,128)(2,1)} %bitcast.8) | data formatting | bytes 50331648 | tf_op jit(solution)/shard_map/all_to_all | solution.py:27
  677.4 9.9 %fusion.16 = f32[24,2048]{1,0:T(8,128)S(1)} fusion(bf16[24,6144]{1,0:T(8,128)(2,1)S(1)} %reshape.53, bf16[6144,2048]{1,0:T(8,128)(2,1)} %bitcast.34), kind=kOutput, calls=%fused_computation.25 | convolution fusion | flops 603979776 | bytes 25657344 | tf_op jit(solution)/shard_map/dot_general | solution.py:30
  687.3 0.0 copy-start.1
  687.3 10.0 %fusion.3 = bf16[24,2048]{1,0:T(8,128)(2,1)S(1)} fusion(bf16[24,6144]{1,0:T(8,128)(2,1)S(1)} %reshape.53, bf16[6144,2048]{1,0:T(8,128)(2,1)} %bitcast.35, f32[24,2048]{1,0:T(8,128)S(1)} %fusion.16), kind=kOutput, calls=%fused_computation.5 | convolution fusion | flops 604274688 | bytes 25755648 | tf_op jit(solution)/shard_map/dot_general | solution.py:31
  697.3 5.3 all_gather.7
  702.6 0.1 dot_general.24
  702.8 11.3 %fusion = f32[2,4,3,3072]{3,0,2,1:T(2,128)} fusion(bf16[1,4096,3072]{2,1,0:T(8,128)(2,1)} %param.11, bf16[2,4,3,4096]{3,2,1,0:T(4,128)(2,1)S(1)} %dot_general.24), kind=kOutput, calls=%fused_computation | convolution fusion | flops 603979776 | bytes 25657344 | tf_op jit(solution)/shard_map/dot_general | solution.py:34
  714.1 0.0 all-reduce.3.cloned.1.call-update
  714.1 36.5 %all-reduce.3.cloned.1.call-done = f32[2,4,3,3072]{3,0,2,1:T(2,128)} async-done(((f32[2,4,3,3072]{3,0,2,1:T(2,128)}), f32[2,4,3,3072]{3,0,2,1:T(2,128)}) %all-reduce.3.cloned.1.call-update) | async-done | bytes 294928
  750.6 1.5 constant_dynamic-slice_fusion
  752.1 0.7 copy.42
  752.8 3.3 all-to-all-start.2
  756.1 0.0 reduce-scatter.2.cloned.1.call-start
  756.2 0.1 convolution_bitcast_fusion
  756.3 0.1 dynamic_slice.7
  756.4 3.9 all-to-all-done.2
  760.4 1.2 fusion.5
  761.6 0.0 reduce-scatter.2.cloned.1.call-update
  761.6 52.8 %reduce-scatter.2.cloned.1.call-done = f32[16,384]{1,0:T(8,128)} async-done(((f32[16,6144]{1,0:T(8,128)}), f32[16,384]{1,0:T(8,128)}) %reduce-scatter.2.cloned.1.call-update) | async-done | bytes 24592 | tf_op jit(solution)/shard_map/reduce_scatter | solution.py:50
  814.4 1.3 convert_element_type.25
  815.8 0.0 copy-done.1
  (8 shorter events, 0.2 us)
Async XLA Ops:
  6.5 330.3 %copy-start = (bf16[16,6144]{1,0:T(8,128)(2,1)S(1)}, bf16[16,6144]{1,0:T(8,128)(2,1)}, u32[]{:S(2)}) copy-start(bf16[16,6144]{1,0:T(8,128)(2,1)} %param.6) | copy-start | bytes 589828
  39.2 285.3 %all-to-all-start = ((bf16[3072,2,2048]{0,2,1:T(8,128)(2,1)}), bf16[3072,2,2048]{0,2,1:T(8,128)(2,1)}, u32[]{:S(2)}, u32[]{:S(2)}) async-start(bf16[3072,2,2048]{0,2,1:T(8,128)(2,1)} %bitcast.37), calls=%async_computation | async-start | bytes 50331648 | tf_op jit(solution)/shard_map/all_to_all | solution.py:26
  324.5 12.0 %copy-start.2 = (s32[16,2]{0,1:T(2,128)S(1)}, s32[16,2]{0,1:T(2,128)}, u32[]{:S(2)}) copy-start(s32[16,2]{0,1:T(2,128)} %param.7) | copy-start | bytes 388
  324.5 288.0 %copy-start.4 = (u32[32]{0:T(128)S(1)}, u32[32]{0:T(128)}, u32[]{:S(2)}) copy-start(u32[32]{0:T(128)} %constant.30) | copy-start | bytes 388
  324.5 288.5 %copy-start.3 = (s32[16,2]{0,1:T(2,128)S(1)}, s32[16,2]{0,1:T(2,128)}, u32[]{:S(2)}) copy-start(s32[16,2]{0,1:T(2,128)} %param.8) | copy-start | bytes 388
  324.5 320.2 %all-to-all-start.1 = ((bf16[3072,2,2048]{0,2,1:T(8,128)(2,1)}), bf16[3072,2,2048]{0,2,1:T(8,128)(2,1)}, u32[]{:S(2)}, u32[]{:S(2)}) async-start(bf16[3072,2,2048]{0,2,1:T(8,128)(2,1)} %bitcast.36), calls=%async_computation.1 | async-start | bytes 50331648 | tf_op jit(solution)/shard_map/all_to_all | solution.py:27
  336.5 414.1 %all-reduce.3.cloned.1.call-start = ((), (), s32[]{:S(2)}) async-start(), calls=%async_computation.5 | async-start | bytes 589824
  687.3 128.5 %copy-start.1 = (bf16[16,6144]{1,0:T(8,128)(2,1)S(1)}, bf16[16,6144]{1,0:T(8,128)(2,1)}, u32[]{:S(2)}) copy-start(bf16[16,6144]{1,0:T(8,128)(2,1)} %param.6) | copy-start | bytes 589828
  752.8 7.5 all-to-all-start.2
  756.1 58.3 %reduce-scatter.2.cloned.1.call-start = ((), (), s32[]{:S(2)}) async-start(), calls=%async_computation.4 | async-start | bytes 417792 | tf_op jit(solution)/shard_map/reduce_scatter | solution.py:50
Sparse Core Ops, SparseCore 0:
  714.2 36.3 all-reduce.2
  761.7 52.6 reduce-scatter.1
where the time goes:
time: 826 us; the launch traced here: 823 us
  waiting for transfers between devices  334 us (40%)
  blocking collectives  281 us (34%)
  local copies, waits for them, and re-layouts  133 us (16%)
  matrix products  32.7 us (4%)
  starting transfers between devices  27.1 us (3%)
  between operations  13.5 us (2%)
    all_gather x1, blocking collectives, per_device(): piece = lax.all_gather(outgoing, 'gy', axis=0, tiled=True)  275 us
    all_to_all x1, waiting for transfers between devices, per_device(): lax.all_to_all(w_gate[0], 'gy', split_axis=1, concat_axis=0, tiled=True)  241 us
    unnamed x16, local copies, waits for them, and re-layouts  67.6 us
    reduce_scatter x1, waiting for transfers between devices, per_device(): lax.psum_scatter(contribution, ('gx', 'gz'), scatter_dimension=1, tiled=T...  52.8 us
    unnamed x3, waiting for transfers between devices  36.5 us
    all_to_all x1, local copies, waits for them, and re-layouts, per_device(): lax.all_to_all(w_up[0], 'gy', split_axis=1, concat_axis=0, tiled=True)  32.7 us
    all_to_all x1, local copies, waits for them, and re-layouts, per_device(): lax.all_to_all(w_gate[0], 'gy', split_axis=1, concat_axis=0, tiled=True)  31.6 us
  transfers between devices with their start and end apart: 5, of which 4 were waited for; matrix products, arithmetic and copies ran while one was open for 8% of the time, Pallas kernels for 0%

commit v1 on v0

--- a/solution.py
+++ b/solution.py
@@ -4,6 +4,12 @@
 from jax.sharding import PartitionSpec as P
 
 CAP = 12
+
+
+def swap_blocks(x, axis, split, join):
+    shards = jnp.split(x, lax.axis_size(axis), axis=split)
+    received = lax.all_to_all(jnp.stack(shards), axis, 0, 0)
+    return jnp.concatenate(received, axis=join)
 
 
 def per_device(tokens, route, weight_q, w_gate, w_up, w_down):
@@ -23,7 +29,7 @@
     token_gate = jnp.sum(hits.astype(jnp.float32) * shares, axis=1)
     slot_gate = jnp.dot(place_full, token_gate, precision=lax.Precision.HIGHEST)
     gate_slab, up_slab = (
-        lax.all_to_all(w_gate[0], "gy", split_axis=1, concat_axis=0, tiled=True),
+        swap_blocks(w_gate[0], "gy", 1, 0),
         lax.all_to_all(w_up[0], "gy", split_axis=1, concat_axis=0, tiled=True),
     )
     piece = lax.all_gather(outgoing, "gy", axis=0, tiled=True)

time: 826 us -> 792 us (0.959)
  local copies, waits for them, and re-layouts: 133 us -> 77.5 us
  waiting for transfers between devices: 334 us -> 347 us
  other arithmetic: 1.57 us -> 11.6 us
    all_to_all x1, waiting for transfers between devices: 0.01 us -> 254 us  [per_device(): lax.all_to_all(w_up[0], 'gy', split_axis=1, concat_axis=0, tiled=True)]
    all_to_all x1, waiting for transfers between devices: 241 us -> 0.01 us  [swap_blocks(): received = lax.all_to_all(jnp.stack(shards), axis, 0, 0)]
    unnamed x16 -> x13, local copies, waits for them, and re-layouts: 67.6 us -> 35 us
    all_to_all x1 -> x0, local copies, waits for them, and re-layouts: 31.6 us -> none  [per_device(): lax.all_to_all(w_gate[0], 'gy', split_axis=1, concat_axis=0, tiled=True)]
    another operation x1 -> x2, other arithmetic: 0.04 us -> 10.1 us  [the longest x1 10 us: swap_blocks(): received = lax.all_to_all(jnp.stack(shards), axis, 0, 0)]
    another operation x1 -> x2, local copies, waits for them, and re-layouts: 0.09 us -> 10 us  [the longest x1 9.91 us: swap_blocks(): received = lax.all_to_all(jnp.stack(shards), axis, 0, 0)]
  transfers between devices with their start and end apart: 5 -> 5, of which waited for: 4 -> 4; matrix products, arithmetic and copies ran while one was open for 8% -> 7% of each run, Pallas kernels for 0% -> 0%
where the time goes in v1:
time: 792 us; the launch traced here: 790 us
  waiting for transfers between devices  347 us (44%)
  blocking collectives  281 us (35%)
  local copies, waits for them, and re-layouts  77.5 us (10%)
  matrix products  32.7 us (4%)
  starting transfers between devices  26.9 us (3%)
  between operations  13.5 us (2%)
  other arithmetic  11.6 us (1%)
    all_gather x1, blocking collectives, per_device(): piece = lax.all_gather(outgoing, 'gy', axis=0, tiled=True)  275 us
    all_to_all x1, waiting for transfers between devices, per_device(): lax.all_to_all(w_up[0], 'gy', split_axis=1, concat_axis=0, tiled=True)  254 us
    reduce_scatter x1, waiting for transfers between devices, per_device(): lax.psum_scatter(contribution, ('gx', 'gz'), scatter_dimension=1, tiled=T...  52.9 us
    unnamed x3, waiting for transfers between devices  36.5 us
    unnamed x13, local copies, waits for them, and re-layouts  35 us
    all_to_all x1, local copies, waits for them, and re-layouts, per_device(): lax.all_to_all(w_up[0], 'gy', split_axis=1, concat_axis=0, tiled=True)  31.6 us
  transfers between devices with their start and end apart: 5, of which 4 were waited for; matrix products, arithmetic and copies ran while one was open for 7% of the time, Pallas kernels for 0%

profile of v1, /device:TPU:0, one launch (start us, length us, event | category | flops | bytes accessed | tf_op | source)
XLA Modules:
  0.0 789.7 jit_solution(18056481269653233885)
XLA Ops:
  6.5 0.0 copy-start
  6.5 32.7 %copy.30 = bf16[1,3072,4096]{1,2,0:T(8,128)(2,1)} copy(bf16[1,3072,4096]{2,1,0:T(8,128)(2,1)} %param.10) | data formatting | bytes 50331648 | tf_op args[4]
  39.3 11.8 %all-to-all-start.1 = ((bf16[3072,2,2048]{0,2,1:T(8,128)(2,1)}), bf16[3072,2,2048]{0,2,1:T(8,128)(2,1)}, u32[]{:S(2)}, u32[]{:S(2)}) async-start(bf16[3072,2,2048]{0,2,1:T(8,128)(2,1)} %bitcast.38), calls=%async_computation.1 | async-start | bytes 50331648 | tf_op jit(solution)/shard_map/all_to_all | solution.py:33
  51.1 9.9 %slice_bitcast_fusion.1 = (bf16[1,3072,2048]{2,1,0:T(8,128)(2,1)S(1)}, bf16[1,3072,2048]{2,1,0:T(8,128)(2,1)S(1)}) fusion(bf16[3072,4096]{1,0:T(8,128)(2,1)} %bitcast.39), kind=kLoop, calls=%fused_computation.4 | loop fusion | bytes 50331648 | tf_op jit(solution)/shard_map/stack | solution.py:11
  61.0 10.0 %pad_maximum_fusion = bf16[2,3072,2048]{2,1,0:T(8,128)(2,1)} fusion(bf16[1,3072,2048]{2,1,0:T(8,128)(2,1)S(1)} %get-tuple-element.6, bf16[1,3072,2048]{2,1,0:T(8,128)(2,1)S(1)} %get-tuple-element.5), kind=kLoop, calls=%fused_computation | loop fusion | flops 12582912 | bytes 50331648 | tf_op jit(solution)/shard_map/stack | solution.py:11
  71.0 0.0 copy-start.1
  71.0 0.0 copy-start.3
  71.0 0.0 copy-start.2
  71.0 253.6 %all-to-all-done.1 = bf16[3072,2,2048]{0,2,1:T(8,128)(2,1)} async-done(((bf16[3072,2,2048]{0,2,1:T(8,128)(2,1)}), bf16[3072,2,2048]{0,2,1:T(8,128)(2,1)}, u32[]{:S(2)}, u32[]{:S(2)}) %all-to-all-start.1) | async-done | bytes 25165856 | tf_op jit(solution)/shard_map/all_to_all | solution.py:33
  324.6 11.7 %all-to-all-start = ((bf16[2,3072,2048]{2,1,0:T(8,128)(2,1)}), bf16[2,3072,2048]{2,1,0:T(8,128)(2,1)}, u32[]{:S(2)}, u32[]{:S(2)}) async-start(bf16[2,3072,2048]{2,1,0:T(8,128)(2,1)} %pad_maximum_fusion), calls=%async_computation | async-start | bytes 50331648 | tf_op jit(solution)/shard_map/all_to_all | solution.py:11
  336.3 0.0 all-reduce.3.cloned.1.call-start
  336.4 0.0 copy-done.1
  336.4 0.1 copy.29
  336.5 0.1 add_reduce_fusion
  336.6 0.0 copy-done
  336.7 0.2 fusion.2
  336.9 275.4 %all-gather = bf16[2,12,6144]{2,1,0:T(8,128)(2,1)S(1)} all-gather(bf16[1,12,6144]{2,1,0:T(8,128)(2,1)S(1)} %fusion.2), channel_id=1, replica_groups=mesh['gx'=4,'gy'=2,'gz'=4] {'gy'}, dimensions={0}, use_global_device_ids=true | all-gather | bytes 442368 | tf_op jit(solution)/shard_map/all_gather | solution.py:35
  612.2 0.1 reshape.53
  612.3 0.0 copy-done.3
  612.3 0.6 dynamic-slice
  612.9 0.0 copy-done.2
  612.9 31.6 %copy.31 = bf16[2,3072,2048]{2,1,0:T(8,128)(2,1)} copy(bf16[2,3072,2048]{1,2,0:T(8,128)(2,1)} %bitcast.9) | data formatting | bytes 50331648 | tf_op jit(solution)/shard_map/all_to_all | solution.py:33
  644.5 0.0 all-to-all-done
  644.5 9.9 %fusion.16 = f32[24,2048]{1,0:T(8,128)S(1)} fusion(bf16[24,6144]{1,0:T(8,128)(2,1)S(1)} %reshape.53, bf16[6144,2048]{1,0:T(8,128)(2,1)} %bitcast.7), kind=kOutput, calls=%fused_computation.28 | convolution fusion | flops 603979776 | bytes 25657344 | tf_op jit(solution)/shard_map/dot_general | solution.py:36
  654.4 10.0 %fusion.3 = bf16[24,2048]{1,0:T(8,128)(2,1)S(1)} fusion(bf16[24,6144]{1,0:T(8,128)(2,1)S(1)} %reshape.53, bf16[6144,2048]{1,0:T(8,128)(2,1)} %bitcast.37, f32[24,2048]{1,0:T(8,128)S(1)} %fusion.16), kind=kOutput, calls=%fused_computation.8 | convolution fusion | flops 604274688 | bytes 25755648 | tf_op jit(solution)/shard_map/dot_general | solution.py:37
  664.4 5.3 all_gather.7
  669.7 0.1 dot_general.24
  669.8 11.3 %fusion = f32[2,4,3,3072]{3,0,2,1:T(2,128)} fusion(bf16[1,4096,3072]{2,1,0:T(8,128)(2,1)} %param.11, bf16[2,4,3,4096]{3,2,1,0:T(4,128)(2,1)S(1)} %dot_general.24), kind=kOutput, calls=%fused_computation.1 | convolution fusion | flops 603979776 | bytes 25657344 | tf_op jit(solution)/shard_map/dot_general | solution.py:40
  681.1 0.0 all-reduce.3.cloned.1.call-update
  681.2 36.5 %all-reduce.3.cloned.1.call-done = f32[2,4,3,3072]{3,0,2,1:T(2,128)} async-done(((f32[2,4,3,3072]{3,0,2,1:T(2,128)}), f32[2,4,3,3072]{3,0,2,1:T(2,128)}) %all-reduce.3.cloned.1.call-update) | async-done | bytes 294928
  717.6 1.5 constant_dynamic-slice_fusion
  719.2 0.7 copy.34
  719.9 3.3 all-to-all-start.2
  723.2 0.0 reduce-scatter.2.cloned.1.call-start
  723.2 0.1 convolution_bitcast_fusion
  723.4 0.1 dynamic_slice.7
  723.4 3.9 all-to-all-done.2
  727.4 1.2 fusion.5
  728.6 0.0 reduce-scatter.2.cloned.1.call-update
  728.6 52.9 %reduce-scatter.2.cloned.1.call-done = f32[16,384]{1,0:T(8,128)} async-done(((f32[16,6144]{1,0:T(8,128)}), f32[16,384]{1,0:T(8,128)}) %reduce-scatter.2.cloned.1.call-update) | async-done | bytes 24592 | tf_op jit(solution)/shard_map/reduce_scatter | solution.py:56
  781.5 1.3 convert_element_type.25
  (8 shorter events, 0.2 us)
Async XLA Ops:
  6.5 330.1 %copy-start = (bf16[16,6144]{1,0:T(8,128)(2,1)S(1)}, bf16[16,6144]{1,0:T(8,128)(2,1)}, u32[]{:S(2)}) copy-start(bf16[16,6144]{1,0:T(8,128)(2,1)} %param.6) | copy-start | bytes 589828
  39.3 285.3 %all-to-all-start.1 = ((bf16[3072,2,2048]{0,2,1:T(8,128)(2,1)}), bf16[3072,2,2048]{0,2,1:T(8,128)(2,1)}, u32[]{:S(2)}, u32[]{:S(2)}) async-start(bf16[3072,2,2048]{0,2,1:T(8,128)(2,1)} %bitcast.38), calls=%async_computation.1 | async-start | bytes 50331648 | tf_op jit(solution)/shard_map/all_to_all | solution.py:33
  71.0 265.4 %copy-start.1 = (s32[16,2]{0,1:T(2,128)S(1)}, s32[16,2]{0,1:T(2,128)}, u32[]{:S(2)}) copy-start(s32[16,2]{0,1:T(2,128)} %param.7) | copy-start | bytes 388
  71.0 541.3 %copy-start.3 = (u32[32]{0:T(128)S(1)}, u32[32]{0:T(128)}, u32[]{:S(2)}) copy-start(u32[32]{0:T(128)} %constant.30) | copy-start | bytes 388
  71.0 541.9 %copy-start.2 = (s32[16,2]{0,1:T(2,128)S(1)}, s32[16,2]{0,1:T(2,128)}, u32[]{:S(2)}) copy-start(s32[16,2]{0,1:T(2,128)} %param.8) | copy-start | bytes 388
  324.6 319.9 %all-to-all-start = ((bf16[2,3072,2048]{2,1,0:T(8,128)(2,1)}), bf16[2,3072,2048]{2,1,0:T(8,128)(2,1)}, u32[]{:S(2)}, u32[]{:S(2)}) async-start(bf16[2,3072,2048]{2,1,0:T(8,128)(2,1)} %pad_maximum_fusion), calls=%async_computation | async-start | bytes 50331648 | tf_op jit(solution)/shard_map/all_to_all | solution.py:11
  336.3 381.3 %all-reduce.3.cloned.1.call-start = ((), (), s32[]{:S(2)}) async-start(), calls=%async_computation.5 | async-start | bytes 589824
  719.9 7.5 all-to-all-start.2
  723.2 58.3 %reduce-scatter.2.cloned.1.call-start = ((), (), s32[]{:S(2)}) async-start(), calls=%async_computation.4 | async-start | bytes 417792 | tf_op jit(solution)/shard_map/reduce_scatter | solution.py:56
Sparse Core Ops, SparseCore 0:
  681.3 36.3 all-reduce.2
  728.7 52.7 reduce-scatter.1
